TPU v7x, 128 devices: a whole 4x4x4 slice. The times are simulated.
128 devices in a mesh: blk: 4 (over y), mp: 16 (over x, z), kv: 2 (over core).
Axes of the slice: x: 4, y: 4, z: 4, core: 2. Of those that a mesh axis runs over, the one named last changes fastest.
Arguments:
- tokens: bfloat16 [2048, 16384], P(('blk', 'kv'), 'mp'), may hold values from -21 to 21, as said below
- norm_gain: bfloat16 [16384], P('mp'), may hold values from 0.099609375 to 1.8984375
- query_weight: bfloat16 [16384, 16384], P('mp', 'blk'), may hold values from -0.53125 to 0.53125, as said below
- key_weight: bfloat16 [16384, 1024], P('mp', 'blk'), may hold values from -0.03125 to 0.03125, as said below
- documents: int32 [2048], replicated, may hold values from 0 to 3, never falling along the last dimension, each value on 1 to 1024 neighbouring positions
- span_ids: int32 [2048], replicated, may hold values from 0 to 1023, never falling along the last dimension, each value on 1 to 4 neighbouring positions
Outputs:
- span_logmap: float32 [1024, 128, 1024], P('kv', ('blk', 'mp'))
Inputs may be any that keep to these rules, and one draw needn't show every extreme that they name: `tokens`: custom draw; values are real-valued activations. `query_weight`: custom draw of fan-in scale. `key_weight`: custom draw of fan-in scale. `documents`: never falling along the tokens; each of the 4 documents covers 1 to 1024 consecutive tokens, one exactly 1024. `span_ids`: never falling along the tokens; each of the 1024 spans covers 1 to 4 consecutive tokens, one exactly 4.
All inputs are finite; a program needn't handle non-finite values.
Results may differ from a plain program's by a relative error of at most 0.0006.
Values may be sent and summed in bfloat16 or wider, within the bound.
A program may use at most 128 MiB of HBM per device.

v0:
```python
import math

import jax
import jax.numpy as jnp
from jax import lax
from jax.sharding import Mesh
from jax.sharding import PartitionSpec as P

D = 16384
HQ = 128
KVH = 8
HD = 128
DOCS = 4
MP = ("mp_0", "mp_1")
MP_KV = ("mp_0", "mp_1", "kv")
BLK_MP = ("blk", "mp_0", "mp_1")


def by_axis(array, axes):
    for axis in axes:
        array = lax.psum(array, axis)
    return array


def copy_for_each(array, axis):
    copies = jnp.broadcast_to(array, (lax.axis_size(axis), *array.shape))
    return lax.all_to_all(copies, axis, split_axis=0, concat_axis=0, tiled=True)


def laid_out(blocks, dim):
    shape = list(blocks.shape[1:])
    shape[dim] *= blocks.shape[0]
    return jnp.moveaxis(blocks, 0, dim).reshape(shape)


def collect(array, axis, dim):
    blocks = copy_for_each(array, axis)
    return laid_out(blocks, dim)


def split_up(array, dim, peers):
    shape = array.shape
    blocks = array.reshape(*shape[:dim], peers, shape[dim] // peers, *shape[dim + 1 :])
    return jnp.moveaxis(blocks, dim, 0)


def sent_and_summed(array, axis, dim):
    peers = lax.axis_size(axis)
    blocks = lax.all_to_all(split_up(array, dim, peers), axis, 0, 0, tiled=True)
    return jnp.sum(blocks.astype(jnp.float32), axis=0)


def rope_freqs(half_width):
    iota_index = jnp.arange(half_width, dtype=jnp.float32)
    base_freq = jnp.power(500000.0, -iota_index / half_width)
    wavelen = 2.0 * jnp.pi / base_freq
    smooth = (8192.0 / wavelen - 1.0) / 3.0
    blended = (1.0 - smooth) * base_freq / 8.0 + smooth * base_freq
    return jnp.where(
        wavelen < 2048.0, base_freq, jnp.where(wavelen > 8192.0, base_freq / 8.0, blended)
    )


def rotate(vectors, cosine, sine_table):
    half_width = vectors.shape[-1] // 2
    first_half = vectors[..., :half_width]
    second_half = vectors[..., half_width:]
    return jnp.concatenate(
        [
            first_half * cosine - second_half * sine_table,
            second_half * cosine + first_half * sine_table,
        ],
        axis=-1,
    )


def doc_positions(documents):
    onehot = (documents[:, None] == jnp.arange(DOCS, dtype=jnp.int32)[None, :]).astype(jnp.int32)
    counts = jnp.sum(onehot, axis=0)
    starts = jnp.cumsum(counts) - counts
    return jnp.arange(documents.shape[0], dtype=jnp.int32) - jnp.sum(
        onehot * starts[None, :], axis=1
    )


def angles(positions):
    frequency = rope_freqs(HD // 2)
    phase_angle = positions.astype(jnp.float32)[:, None] * frequency[None, :]
    return (jnp.cos(phase_angle), jnp.sin(phase_angle))


def arrange(table, blk_count, kv_count, block_rows):
    trailing = table.shape[1:]
    grouped = table.reshape((blk_count, kv_count, block_rows) + trailing)
    return jnp.swapaxes(grouped, 0, 1).reshape((kv_count, blk_count * block_rows) + trailing)


def local(tokens, norm_gain, query_weight, key_weight, documents, span_ids):
    blk_count = lax.axis_size("blk")
    mp_count = lax.axis_size(MP)
    kv_count = lax.axis_size("kv")
    kv_index = lax.axis_index("kv")
    mp_index = lax.axis_index(MP)
    block_rows = tokens.shape[0]
    half_rows = block_rows * blk_count
    total_rows = half_rows * kv_count
    span_count = total_rows // 2
    per_device = query_weight.shape[1] // HD // mp_count
    kv_local = mp_index * per_device // (HQ // KVH)
    activations = tokens.astype(jnp.float32)
    row_squares = by_axis(jnp.sum(activations * activations, axis=1), MP)
    normed = (
        activations
        * lax.rsqrt(row_squares / D + 1e-05)[:, None]
        * norm_gain.astype(jnp.float32)[None, :]
    ).astype(jnp.bfloat16)
    token_order = jnp.arange(total_rows, dtype=jnp.int32)
    cosine, sine_table = angles(doc_positions(documents))
    half_order = arrange(token_order, blk_count, kv_count, block_rows)
    half_docs = arrange(documents, blk_count, kv_count, block_rows)
    half_spans = arrange(span_ids, blk_count, kv_count, block_rows)
    own_order = lax.dynamic_index_in_dim(half_order, kv_index, 0, keepdims=False)
    own_docs = lax.dynamic_index_in_dim(half_docs, kv_index, 0, keepdims=False)
    own_spans = lax.dynamic_index_in_dim(half_spans, kv_index, 0, keepdims=False)
    own_cosine = lax.dynamic_index_in_dim(
        arrange(cosine, blk_count, kv_count, block_rows), kv_index, 0, keepdims=False
    )
    own_sine = lax.dynamic_index_in_dim(
        arrange(sine_table, blk_count, kv_count, block_rows), kv_index, 0, keepdims=False
    )
    gathered = collect(normed, "blk", 0)
    product = jnp.dot(gathered, query_weight, preferred_element_type=jnp.float32)
    query_raw = lax.psum_scatter(
        jnp.transpose(
            product.reshape(half_rows, lax.axis_size(MP) * per_device, HD), (1, 0, 2)
        ).astype(jnp.bfloat16),
        MP,
        scatter_dimension=0,
        tiled=True,
    ).astype(jnp.float32)
    key_partial = jnp.dot(gathered, key_weight, preferred_element_type=jnp.float32)
    queries = rotate(query_raw, own_cosine[None, :, :], own_sine[None, :, :]).astype(jnp.bfloat16)
    share_rows = half_rows // mp_count
    key_share = sent_and_summed(key_partial.astype(jnp.bfloat16), MP, 0)
    share_cosine = lax.dynamic_slice_in_dim(own_cosine, mp_index * share_rows, share_rows, 0)
    share_sine = lax.dynamic_slice_in_dim(own_sine, mp_index * share_rows, share_rows, 0)
    share_heads = key_share.reshape(share_rows, -1, HD)
    key_rotated = (
        rotate(share_heads, share_cosine[:, None, :], share_sine[:, None, :])
        .astype(jnp.bfloat16)
        .reshape(share_rows, -1)
    )
    key_gathered = collect(key_rotated, MP_KV, 0)
    key_block = lax.dynamic_slice_in_dim(key_gathered, kv_local * HD, HD, 1)

    def regroup(table):
        return jnp.swapaxes(table.reshape(kv_count, mp_count, share_rows), 0, 1).reshape(-1)

    key_order = regroup(half_order)
    key_docs = regroup(half_docs)
    key_spans = regroup(half_spans)
    visible = (own_docs[:, None] == key_docs[None, :]) & (key_order[None, :] <= own_order[:, None])
    scores = jnp.einsum("hqd,kd->hqk", queries, key_block, preferred_element_type=jnp.float32) * (
        1.0 / math.sqrt(HD)
    )
    peak_score = jnp.max(jnp.where(visible[None], scores, -jnp.inf), axis=2, keepdims=True)
    weights = jnp.exp(jnp.where(visible[None], scores - peak_score, -jnp.inf))
    attn_probs = (weights / jnp.sum(weights, axis=2, keepdims=True)).astype(jnp.bfloat16)
    span_iota = jnp.arange(span_count, dtype=jnp.int32)
    key_onehot = (key_spans[:, None] == span_iota[None, :]).astype(jnp.bfloat16)
    key_mass = jnp.einsum(
        "hqk,ks->hqs", attn_probs, key_onehot, preferred_element_type=jnp.float32
    ).astype(jnp.bfloat16)
    query_onehot = (own_spans[:, None] == span_iota[None, :]).astype(jnp.bfloat16)
    partial_total = jnp.einsum(
        "qa,hqs->ahs", query_onehot, key_mass, preferred_element_type=jnp.float32
    )
    span_total = sent_and_summed(partial_total.astype(jnp.bfloat16), "kv", 0)
    span_counts = jnp.sum((span_ids[:, None] == span_iota[None, :]).astype(jnp.float32), axis=0)
    own_rows = span_count // kv_count
    own_counts = lax.dynamic_slice_in_dim(span_counts, kv_index * own_rows, own_rows, 0)
    return jnp.log(span_total / own_counts[:, None, None] + 1e-06)


def solution(mesh):
    finer = Mesh(
        mesh.devices.reshape(mesh.shape["blk"], 4, 4, mesh.shape["kv"]),
        ("blk", "mp_0", "mp_1", "kv"),
    )
    return jax.shard_map(
        local,
        mesh=finer,
        in_specs=(P(("blk", "kv"), MP), P(MP), P(MP, "blk"), P(MP, "blk"), P(), P()),
        out_specs=P("kv", BLK_MP, None),
        check_vma=False,
    )
```

profile of v0, /device:TPU:1, one launch (start us, length us, event | category | flops | bytes accessed | tf_op | source)
XLA Modules:
  0.0 225.9 jit_solution(1620455508299441479)
XLA Ops:
  6.5 0.0 copy-start
  6.5 1.3 fusion.30
  7.8 9.3 %psum.14 = f32[256]{0:T(256)S(1)} all-reduce(f32[256]{0:T(256)S(1)} %fusion.30), channel_id=1, replica_groups=mesh['blk'=4,'mp_0'=4,'mp_1'=4,'kv'=2] {'mp_0'}, use_global_device_ids=true, to_apply=%region_1.2 | all-reduce | flops 256 | bytes 2048 | tf_op jit(solution)/shard_map/psum | solution.py:21
  17.1 9.7 %psum.15 = f32[256]{0:T(256)S(1)} all-reduce(f32[256]{0:T(256)S(1)} %psum.14), channel_id=1, replica_groups=mesh['blk'=4,'mp_0'=4,'mp_1'=4,'kv'=2] {'mp_1'}, use_global_device_ids=true, to_apply=%region_2.3 | all-reduce | flops 256 | bytes 2048 | tf_op jit(solution)/shard_map/psum | solution.py:21
  26.9 0.7 convert_element_type.58
  27.5 1.2 fusion.32
  28.8 1.6 broadcast_in_dim.17
  30.4 4.2 %all-to-all-start = ((bf16[4,256,1024]{2,1,0:T(8,128)(2,1)}), bf16[4,256,1024]{2,1,0:T(8,128)(2,1)S(1)}, u32[]{:S(2)}, u32[]{:S(2)}) async-start(bf16[4,256,1024]{2,1,0:T(8,128)(2,1)} %broadcast_in_dim.17), calls=%async_computation | async-start | bytes 4194304 | tf_op jit(solution)/shard_map/all_to_all | solution.py:27
  34.6 0.0 reduce-scatter.2.cloned.1.call-start
  34.6 11.9 %copy.32 = bf16[4096,1024]{1,0:T(8,128)(2,1)} copy(bf16[4096,1024]{0,1:T(8,128)(2,1)} %bitcast.85) | data formatting | bytes 16777216 | tf_op jit(solution)/shard_map/dot_general | solution.py:132
  46.5 9.5 %all-to-all-done = bf16[4,256,1024]{2,1,0:T(8,128)(2,1)S(1)} async-done(((bf16[4,256,1024]{2,1,0:T(8,128)(2,1)}), bf16[4,256,1024]{2,1,0:T(8,128)(2,1)S(1)}, u32[]{:S(2)}, u32[]{:S(2)}) %all-to-all-start) | async-done | bytes 2097184 | tf_op jit(solution)/shard_map/all_to_all | solution.py:27
  56.0 0.0 copy-start.2
  56.0 13.2 %convert_bitcast_fusion = bf16[32,1024,128]{2,1,0:T(8,128)(2,1)} fusion(bf16[1024,1024,1]{1,0,2:T(8,128)(2,1)S(1)} %bitcast.88, bf16[32,128,1024]{2,1,0:T(8,128)(2,1)} %bitcast.86), kind=kOutput, calls=%fused_computation.12 | convolution fusion | flops 8594128896 | bytes 18874368 | tf_op jit(solution)/shard_map/dot_general | solution.py:132
  69.2 0.0 copy-done.2
  69.2 0.0 copy-start.3
  69.2 0.0 copy-start.4
  69.2 0.0 reduce-scatter.2.cloned.1.call-update
  69.3 0.7 copy-done.3
  69.9 0.1 convert_reduce_fusion.3
  70.1 0.2 reduce-window.8
  70.3 0.1 select_reduce_fusion.1
  70.5 0.1 reshape_reshape.7
  70.5 0.1 eq.83
  70.6 0.1 reshape.257
  70.7 0.1 add_add_fusion
  70.8 0.1 reshape.259
  70.9 0.0 copy-done.4
  70.9 0.1 reshape_reshape.8
  71.0 0.1 eq.89
  71.1 1.0 convert_reduce_fusion
  72.1 0.1 dynamic_slice.37
  72.2 3.7 %multiply_cosine_fusion = (f32[2,1024,64]{2,1,0:T(8,128)S(1)}, f32[2,1024,64]{2,1,0:T(8,128)S(1)}) fusion(f32[64]{0:T(128)S(1)} %compare_select_fusion.1, f32[2,1024]{1,0:T(2,128)S(1)} %bitcast.98), kind=kLoop, calls=%fused_computation.27 | loop fusion | flops 131072 | bytes 1057024 | tf_op jit(solution)/shard_map/cos | solution.py:89
  75.9 0.0 copy-done
  75.9 3.2 %convolution_convert_fusion = bf16[1024,256]{1,0:T(8,128)(2,1)} fusion(bf16[1024,1024]{1,0:T(8,128)(2,1)} %bitcast.89, bf16[1024,256]{1,0:T(8,128)(2,1)S(1)} %copy-done), kind=kOutput, calls=%fused_computation.30 | convolution fusion | flops 537133056 | bytes 3145728 | tf_op jit(solution)/shard_map/dot_general | solution.py:141
  79.1 3.6 %all-to-all-start.1 = ((bf16[16,64,256]{2,1,0:T(8,128)(2,1)}), bf16[16,64,256]{2,1,0:T(8,128)(2,1)S(1)}, u32[]{:S(2)}, u32[]{:S(2)}) async-start(bf16[16,64,256]{2,1,0:T(8,128)(2,1)} %bitcast.21), calls=%async_computation.2 | async-start | bytes 1048576 | tf_op jit(solution)/shard_map/all_to_all | solution.py:49
  82.7 1.8 fusion.74
  84.5 9.7 %all-to-all-done.1 = bf16[16,64,256]{2,1,0:T(8,128)(2,1)S(1)} async-done(((bf16[16,64,256]{2,1,0:T(8,128)(2,1)}), bf16[16,64,256]{2,1,0:T(8,128)(2,1)S(1)}, u32[]{:S(2)}, u32[]{:S(2)}) %all-to-all-start.1) | async-done | bytes 524320 | tf_op jit(solution)/shard_map/all_to_all | solution.py:49
  94.2 0.1 convert_reduce_fusion.2
  94.3 0.2 subtract_convert_fusion.1
  94.5 0.1 pad_maximum_fusion.5
  94.6 1.1 broadcast_in_dim.18
  95.7 11.3 %all-to-all-start.2 = ((bf16[32,64,256]{2,1,0:T(8,128)(2,1)}), bf16[32,64,256]{2,1,0:T(8,128)(2,1)}, u32[]{:S(2)}, u32[]{:S(2)}) async-start(bf16[32,64,256]{2,1,0:T(8,128)(2,1)} %broadcast_in_dim.18), calls=%async_computation.3 | async-start | bytes 2097152 | tf_op jit(solution)/shard_map/all_to_all | solution.py:27
  107.1 0.1 dynamic-slice_bitcast_fusion
  107.1 2.5 %compare_and_fusion = pred[1024,2048]{1,0:T(8,128)(4,1)S(1)} fusion(s32[2048]{0:T(1024)S(1)} %reshape.259, s32[2048]{0:T(1024)S(1)} %eq.83, s32[1024]{0:T(1024)S(1)} %bitcast.101, s32[1024]{0:T(1024)S(1)} %bitcast.102), kind=kLoop, calls=%fused_computation.16 | loop fusion | flops 6291456 | bytes 2121728 | tf_op jit(solution)/shard_map/and | solution.py:162
  109.7 56.0 %reduce-scatter.2.cloned.1.call-done = bf16[2,1024,128]{2,1,0:T(8,128)(2,1)} async-done(((bf16[32,1024,128]{2,1,0:T(8,128)(2,1)}), bf16[2,1024,128]{2,1,0:T(8,128)(2,1)}) %reduce-scatter.2.cloned.1.call-update) | async-done | bytes 524304 | tf_op jit(solution)/shard_map/reduce_scatter | solution.py:133
  165.7 1.1 convert_element_type.62
  166.8 1.5 subtract_convert_fusion
  168.3 0.0 all-to-all-done.2
  168.3 13.7 %fusion.56 = (f32[2,1024]{1,0:T(2,128)S(1)}, f32[2,1024,2048]{2,1,0:T(8,128)}) fusion(pred[1024,2048]{1,0:T(8,128)(4,1)S(1)} %compare_and_fusion, bf16[2048,256]{1,0:T(8,128)(2,1)} %bitcast.24, s32[]{:T(128)S(6)} %select_n.57, bf16[2,1024,64]{2,1,0:T(8,128)(2,1)} %get-tuple-element.6, bf16[2,1024,64]{2,1,0:T(8,128)(2,1)} %get-tuple-element.5), kind=kOutput, calls=%fused_computation.75 | convolution fusion | flops 2174748672 | bytes 24126464 | tf_op jit(solution)/shard_map/sub | solution.py:167
  182.0 18.7 %fusion.20 = bf16[1024,2,1024]{2,0,1:T(8,128)(2,1)} fusion(s32[2048]{0:T(1024)S(1)} %eq.89, f32[2,1024,2048]{2,1,0:T(8,128)} %get-tuple-element.12, f32[2,1024]{1,0:T(2,128)S(1)} %get-tuple-element.11, pred[1024,1024,1]{0,1,2:T(32,128)(4,1)} %fusion.74), kind=kOutput, calls=%fused_computation.23 | convolution fusion | flops 12899581952 | bytes 22036480 | tf_op jit(solution)/shard_map/qa,hqs->ahs/dot_general | solution.py:175
  200.7 2.6 %copy.29 = bf16[2,512,2,1024]{3,1,2,0:T(8,128)(2,1)S(1)} copy(bf16[2,512,2,1024]{3,1,0,2:T(8,128)(2,1)} %bitcast.87) | data formatting | bytes 8388608 | tf_op jit(solution)/shard_map/reshape | solution.py:43
  203.3 8.8 %all_to_all.20 = bf16[2,512,2,1024]{3,1,2,0:T(8,128)(2,1)S(1)} all-to-all(bf16[2,512,2,1024]{3,1,2,0:T(8,128)(2,1)S(1)} %copy.29), channel_id=1, replica_groups=mesh['blk'=4,'mp_0'=4,'mp_1'=4,'kv'=2] {'kv'}, dimensions={0} | all-to-all | bytes 8388608 | tf_op jit(solution)/shard_map/all_to_all | solution.py:49
  212.1 0.0 copy-start.1
  212.1 1.0 convert_reduce_fusion.1
  213.1 0.7 add_log_fusion
  213.8 5.2 %copy.31 = f32[512,2,1024]{2,1,0:T(2,128)} copy(f32[512,2,1024]{2,0,1:T(8,128)S(1)} %add_log_fusion) | data formatting | bytes 8388608 | tf_op jit(solution)/shard_map/log | solution.py:182
  219.1 0.0 copy-done.1
  (23 shorter events, 0.2 us)
Async XLA Ops:
  6.5 69.4 %copy-start = (bf16[1024,256]{1,0:T(8,128)(2,1)S(1)}, bf16[1024,256]{1,0:T(8,128)(2,1)}, u32[]{:S(2)}) copy-start(bf16[1024,256]{1,0:T(8,128)(2,1)} %param.9) | copy-start | bytes 1572868
  30.4 25.6 %all-to-all-start = ((bf16[4,256,1024]{2,1,0:T(8,128)(2,1)}), bf16[4,256,1024]{2,1,0:T(8,128)(2,1)S(1)}, u32[]{:S(2)}, u32[]{:S(2)}) async-start(bf16[4,256,1024]{2,1,0:T(8,128)(2,1)} %broadcast_in_dim.17), calls=%async_computation | async-start | bytes 4194304 | tf_op jit(solution)/shard_map/all_to_all | solution.py:27
  34.6 131.2 %reduce-scatter.2.cloned.1.call-start = ((), (), s32[]{:S(2)}) async-start(), calls=%async_computation.5 | async-start | bytes 8912896 | tf_op jit(solution)/shard_map/reduce_scatter | solution.py:133
  56.0 13.2 %copy-start.2 = (bf16[4,256,1024]{2,1,0:T(8,128)(2,1)}, bf16[4,256,1024]{2,1,0:T(8,128)(2,1)S(1)}, u32[]{:S(2)}) copy-start(bf16[4,256,1024]{2,1,0:T(8,128)(2,1)S(1)} %all-to-all-done) | copy-start | bytes 6291460
  69.2 0.7 copy-start.3
  69.2 1.7 copy-start.4
  79.1 15.1 %all-to-all-start.1 = ((bf16[16,64,256]{2,1,0:T(8,128)(2,1)}), bf16[16,64,256]{2,1,0:T(8,128)(2,1)S(1)}, u32[]{:S(2)}, u32[]{:S(2)}) async-start(bf16[16,64,256]{2,1,0:T(8,128)(2,1)} %bitcast.21), calls=%async_computation.2 | async-start | bytes 1048576 | tf_op jit(solution)/shard_map/all_to_all | solution.py:49
  95.7 72.6 %all-to-all-start.2 = ((bf16[32,64,256]{2,1,0:T(8,128)(2,1)}), bf16[32,64,256]{2,1,0:T(8,128)(2,1)}, u32[]{:S(2)}, u32[]{:S(2)}) async-start(bf16[32,64,256]{2,1,0:T(8,128)(2,1)} %broadcast_in_dim.18), calls=%async_computation.3 | async-start | bytes 2097152 | tf_op jit(solution)/shard_map/all_to_all | solution.py:27
  212.1 7.0 %copy-start.1 = (bf16[1024,256]{1,0:T(8,128)(2,1)S(1)}, bf16[1024,256]{1,0:T(8,128)(2,1)}, u32[]{:S(2)}) copy-start(bf16[1024,256]{1,0:T(8,128)(2,1)} %param.9) | copy-start | bytes 1572868
Sparse Core Ops, SparseCore 0:
  69.4 96.2 reduce-scatter.1
where the time goes:
time: 227 us; the launch traced here: 226 us
  waiting for transfers between devices  75.2 us (33%)
  matrix products  48.8 us (21%)
  blocking collectives  27.8 us (12%)
  local copies, waits for them, and re-layouts  24 us (11%)
  starting transfers between devices  19.1 us (8%)
  other arithmetic  17.4 us (8%)
  between operations  13.7 us (6%)
    reduce_scatter x1, waiting for transfers between devices, local(): lax.psum_scatter(jnp.transpose(product.reshape(half_rows, lax.axis_size(M...  56 us
    psum x2, blocking collectives, by_axis(): array = lax.psum(array, axis)  19 us
    dot_general x1, matrix products, local(): jnp.einsum('qa,hqs->ahs', query_onehot, key_mass, preferred_element_type=...  18.7 us
    all_to_all x2, starting transfers between devices, copy_for_each(): return lax.all_to_all(copies, axis, split_axis=0, concat_axis=0, tiled=True)  15.5 us
    sub x1, matrix products, local(): weights = jnp.exp(jnp.where(visible[None], scores - peak_score, -jnp.inf))  13.7 us
    dot_general x1, matrix products, local(): jnp.dot(gathered, query_weight, preferred_element_type=jnp.float32)  13.2 us
    dot_general x1, local copies, waits for them, and re-layouts, local(): jnp.dot(gathered, query_weight, preferred_element_type=jnp.float32)  11.9 us
    all_to_all x1, waiting for transfers between devices, sent_and_summed(): blocks = lax.all_to_all(split_up(array, dim, peers), axis, 0, 0, tiled=True)  9.65 us
  transfers between devices with their start and end apart: 4, of which 3 were waited for; matrix products, arithmetic and copies ran while one was open for 13% of the time, Pallas kernels for 0%

commit v1 on v0

v1 whole, which is shorter than its diff:
```python
import functools
import math

import jax
import jax.numpy as jnp
import numpy as np
from jax import lax
from jax.experimental import pallas as pl
from jax.experimental.pallas import tpu as pltpu
from jax.sharding import Mesh
from jax.sharding import PartitionSpec as P

D = 16384
HD = 128
TOKENS = 2048
NS = 1024
X, Z, Y, CORE = "mp_0", "mp_1", "blk", "kv"
MP = (X, Z)
BLK_MP = (Y, X, Z)
MESH = pl.DeviceIdType.MESH
F32 = jnp.float32
BF16 = jnp.bfloat16
RING = 4
CH = 8
R = 128
KI = 4
LAST = CH + 4
SLOT_A = {2: 0, 1: 2, 3: 1, 0: 3}
SLOT_B = {2: 1, 1: 0, 3: 2, 0: 3}
ORDER = (2, 1, 3, 0)
PEERS = [(ox, oz) for ox in range(4) for oz in range(4) if (ox, oz) != (0, 0)]


def step(pos, by):
    return lax.rem(pos + by, RING)


def piece_of(i):
    half = lax.rem(i + i // 4 + i // 6, 2)
    far = i // 6
    other = (i + 4) // 6
    offset = other * (1 - far) * (3 - 2 * lax.rem(i, 2)) + 2 * far
    return offset, half


def first_send(st, r, ssem, rsem, axis, d):
    target = step(lax.axis_index(axis), 1 if d == 0 else 3)
    return pltpu.make_async_remote_copy(
        src_ref=st.at[d],
        dst_ref=r.at[d],
        send_sem=ssem.at[0, d],
        recv_sem=rsem.at[0, d],
        device_id={axis: target},
        device_id_type=MESH,
    )


def second_send(st, rb, ssem, rsem, axis, d):
    h = st.shape[1] // 2
    target = step(lax.axis_index(axis), 1 if d == 0 else 3)
    rows = pl.ds(d * h, h)
    return pltpu.make_async_remote_copy(
        src_ref=st.at[2, rows],
        dst_ref=rb.at[rows],
        send_sem=ssem.at[1, d],
        recv_sem=rsem.at[1, d],
        device_id={axis: target},
        device_id_type=MESH,
    )


def add_far(st, r):
    h = st.shape[1] // 2
    st[2, :h] = (st[2, :h].astype(F32) + r[0, :h].astype(F32)).astype(BF16)
    st[2, h:] = (st[2, h:].astype(F32) + r[1, h:].astype(F32)).astype(BF16)


def total_of(st, r, rb, lo, n):
    h = st.shape[1] // 2
    lanes = pl.ds(lo, n)
    top = st[3, :h, lanes].astype(F32) + r[1, :h, lanes].astype(F32) + rb[:h, lanes].astype(F32)
    low = st[3, h:, lanes].astype(F32) + r[0, h:, lanes].astype(F32) + rb[h:, lanes].astype(F32)
    return top.astype(BF16), low.astype(BF16)


def put(st, offset, lo, n, top, low):
    h = st.shape[1] // 2
    st[SLOT_A[offset], :h, lo : lo + n] = top
    st[SLOT_B[offset], h:, lo : lo + n] = low


def project_kernel(
    tok_hbm, gain_ref, w_hbm, kw_hbm, q_out, k_out, ssq_out,
    tok, xs, wbuf, kwbuf, st1, r1, r1b, st2, r2, r2b,
    kpart, kst1, kr1, kr1b, kst2, kr2, kr2b, kfin,
    ssq_own, ssq_in, ssq_sum, ssq_far,
    load_sem, w_sem, g_send, g_recv, s_send, s_recv, k_send, k_recv,
    a_send, a_recv, n_send, n_recv, d_send, d_recv, e_send, e_recv,
):
    x, z, y, core = (lax.axis_index(a) for a in (X, Z, Y, CORE))
    axes = (X, Z)
    barrier = pltpu.get_barrier_semaphore()
    for ox, oz in PEERS:
        pl.semaphore_signal(barrier, 1, device_id={X: step(x, ox), Z: step(z, oz)}, device_id_type=MESH)
    for by in (1, 3):
        pl.semaphore_signal(barrier, 1, device_id={Y: step(y, by)}, device_id_type=MESH)
    pl.semaphore_signal(barrier, 1, device_id={CORE: 1 - core}, device_id_type=MESH)

    def tok_load(p):
        return pltpu.make_async_copy(tok_hbm.at[pl.ds(p * R, R)], tok.at[p], load_sem.at[p])

    def w_load(ox, oz):
        col = (step(x, ox) * 4 + step(z, oz)) * 256
        return pltpu.make_async_copy(
            w_hbm.at[:, pl.ds(pl.multiple_of(col, 256), 256)], wbuf.at[ox * 4 + oz], w_sem.at[ox * 4 + oz]
        )

    kw_load = pltpu.make_async_copy(kw_hbm, kwbuf, load_sem.at[2])
    for p in range(2):
        tok_load(p).start()
    for ox in ORDER:
        for oz in ORDER:
            w_load(ox, oz).start()
    kw_load.start()

    def scale(p):
        xs[p] = (tok[p].astype(F32) * gain_ref[...].astype(F32)).astype(BF16)

    def gather(n, src, dst, by):
        return pltpu.make_async_remote_copy(
            src_ref=tok.at[src],
            dst_ref=tok.at[dst],
            send_sem=g_send.at[n],
            recv_sem=g_recv.at[n],
            device_id={Y: step(y, by)},
            device_id_type=MESH,
        )

    gathers = [
        gather(0, 0, 2, 1), gather(1, 1, 3, 3), gather(2, 1, 4, 1),
        gather(3, 0, 5, 3), gather(4, 2, 6, 1), gather(5, 3, 7, 3),
    ]
    for p in range(2):
        tok_load(p).wait()
    pl.semaphore_wait(barrier, len(PEERS) + 3)
    for n in range(4):
        gathers[n].start()
    for p in range(2):
        scale(p)

    def q_first(c, color, stage, d):
        st, r = (st1, r1) if stage == 0 else (st2, r2)
        axis = axes[color] if stage == 0 else axes[1 - color]
        return first_send(
            st.at[color, c], r.at[color, c], s_send.at[c, color, stage], s_recv.at[c, color, stage], axis, d
        )

    def q_second(c, color, stage, d):
        st, rb = (st1, r1b) if stage == 0 else (st2, r2b)
        axis = axes[color] if stage == 0 else axes[1 - color]
        return second_send(
            st.at[color, c], rb.at[color, c], s_send.at[c, color, stage], s_recv.at[c, color, stage], axis, d
        )

    def k_first(color, stage, d):
        st, r = (kst1, kr1) if stage == 0 else (kst2, kr2)
        axis = axes[color] if stage == 0 else axes[1 - color]
        return first_send(st.at[color], r.at[color], k_send.at[color, stage], k_recv.at[color, stage], axis, d)

    def k_second(color, stage, d):
        st, rb = (kst1, kr1b) if stage == 0 else (kst2, kr2b)
        axis = axes[color] if stage == 0 else axes[1 - color]
        return second_send(st.at[color], rb.at[color], k_send.at[color, stage], k_recv.at[color, stage], axis, d)

    mine = x * 4 + z
    k_off, k_half = piece_of(mine // 2)
    k_blk = step(y, k_off)
    k_slot = k_half * 2 + lax.rem(mine, 2)

    def key_send(n):
        ox, oz = PEERS[n]
        return pltpu.make_async_remote_copy(
            src_ref=kfin.at[step(x, ox) // 2],
            dst_ref=k_out.at[k_blk, core, k_slot],
            send_sem=a_send.at[n],
            recv_sem=a_recv.at[n],
            device_id={X: step(x, ox), Z: step(z, oz)},
            device_id_type=MESH,
        )

    def square_send(n):
        ox, oz = PEERS[n]
        return pltpu.make_async_remote_copy(
            src_ref=ssq_own,
            dst_ref=ssq_in.at[n],
            send_sem=n_send.at[n],
            recv_sem=n_recv.at[n],
            device_id={X: step(x, ox), Z: step(z, oz)},
            device_id_type=MESH,
        )

    def q_share(c):
        off, half = piece_of(c)
        part = q_out.at[step(y, off), core, half]
        return pltpu.make_async_remote_copy(
            src_ref=part,
            dst_ref=part,
            send_sem=d_send.at[c],
            recv_sem=d_recv.at[c],
            device_id={CORE: 1 - core},
            device_id_type=MESH,
        )

    k_share = pltpu.make_async_remote_copy(
        src_ref=k_out.at[:, core],
        dst_ref=k_out.at[:, core],
        send_sem=e_send.at[0],
        recv_sem=e_recv.at[0],
        device_id={CORE: 1 - core},
        device_id_type=MESH,
    )
    square_share = pltpu.make_async_remote_copy(
        src_ref=ssq_sum,
        dst_ref=ssq_far,
        send_sem=e_send.at[1],
        recv_sem=e_recv.at[1],
        device_id={CORE: 1 - core},
        device_id_type=MESH,
    )

    def put_squares(src, whose):
        for c in range(CH):
            off, half = piece_of(jnp.int32(c))
            row = step(y, off) * 4 + whose * 2 + half
            ssq_out[pl.ds(row, 1), :] = src[c : c + 1, :]

    both = [(color, d) for color in range(2) for d in range(2)]

    def body(i, carry):
        @pl.when(i == 2)
        def _():
            for n in range(2):
                gathers[n].wait_recv()
                gathers[4 + n].start()
            for p in (2, 3):
                scale(p)

        @pl.when(i == KI)
        def _():
            for n in range(2, 6):
                gathers[n].wait_recv()
            for p in range(4, 8):
                scale(p)

        @pl.when(i < CH)
        def _():
            lhs = xs[i]
            for n, ox in enumerate(ORDER):
                for oz in ORDER:
                    @pl.when(i == 0)
                    def _():
                        w_load(ox, oz).wait()

                    out = jnp.dot(lhs, wbuf[ox * 4 + oz], preferred_element_type=F32).astype(BF16)
                    h = R // 2
                    put(st1.at[0, i], ox, oz * HD, HD, out[:h, :HD], out[h:, :HD])
                    put(st1.at[1, i], oz, ox * HD, HD, out[:h, HD:], out[h:, HD:])
                if n == 1:
                    q_first(i, 0, 0, 0).start()
                if n == 2:
                    q_first(i, 0, 0, 1).start()
            for d in range(2):
                q_first(i, 1, 0, d).start()

        @pl.when(i == KI)
        def _():
            kw_load.wait()
            eye = lax.broadcasted_iota(jnp.int32, (R, R), 0) == lax.broadcasted_iota(jnp.int32, (R, R), 1)

            def one(p, carry):
                kpart[pl.ds(pl.multiple_of(p * R, R), R), :] = jnp.dot(
                    xs[p], kwbuf[...], preferred_element_type=F32
                ).astype(BF16)
                acc = jnp.zeros((R, 128), F32)
                for j in range(8):
                    t = tok[p, :, j * 128 : (j + 1) * 128].astype(F32)
                    acc = acc + t * t
                col = jnp.sum(acc, axis=1, keepdims=True)
                ssq_own[pl.ds(p, 1), :] = jnp.sum(jnp.where(eye, col, 0.0), axis=0, keepdims=True)
                return carry

            lax.fori_loop(0, CH, one, 0)
            for ox in range(4):
                for oz in range(4):
                    row = (step(x, ox) * 4 + step(z, oz)) * 64
                    rows = kpart[pl.ds(pl.multiple_of(row, 64), 64), :]
                    put(kst1.at[0], ox, oz * HD, HD, rows[:32, :HD], rows[32:, :HD])
                    put(kst1.at[1], oz, ox * HD, HD, rows[:32, HD:], rows[32:, HD:])
            for color, d in both:
                k_first(color, 0, d).start()
            for n in range(len(PEERS)):
                square_send(n).start()

        for stage in range(2):
            lag = 1 + 2 * stage

            @pl.when((i >= lag) & (i < CH + lag))
            def _(stage=stage, lag=lag):
                c = i - lag
                for color in range(2):
                    for d in range(2):
                        q_first(c, color, stage, d).wait_recv()
                    add_far((st1 if stage == 0 else st2).at[color, c], (r1 if stage == 0 else r2).at[color, c])
                    for d in range(2):
                        q_second(c, color, stage, d).start()

            @pl.when(i == KI + lag)
            def _(stage=stage):
                for color in range(2):
                    for d in range(2):
                        k_first(color, stage, d).wait_recv()
                    add_far((kst1 if stage == 0 else kst2).at[color], (kr1 if stage == 0 else kr2).at[color])
                    for d in range(2):
                        k_second(color, stage, d).start()

            if stage == 0:
                @pl.when((i >= 2) & (i < CH + 2))
                def _():
                    c = i - 2
                    for color in range(2):
                        for d in range(2):
                            q_second(c, color, 0, d).wait_recv()
                        for o in range(4):
                            top, low = total_of(st1.at[color, c], r1.at[color, c], r1b.at[color, c], o * HD, HD)
                            put(st2.at[color, c], o, 0, HD, top, low)
                        for d in range(2):
                            q_first(c, color, 1, d).start()

                @pl.when(i == KI + 2)
                def _():
                    for color in range(2):
                        for d in range(2):
                            k_second(color, 0, d).wait_recv()
                        for o in range(4):
                            top, low = total_of(kst1.at[color], kr1.at[color], kr1b.at[color], o * HD, HD)
                            put(kst2.at[color], o, 0, HD, top, low)
                        for d in range(2):
                            k_first(color, 1, d).start()

        @pl.when(i >= 4)
        def _():
            c = i - 4
            off, half = piece_of(c)
            blk = step(y, off)
            for color in range(2):
                for d in range(2):
                    q_second(c, color, 1, d).wait_recv()
                top, low = total_of(st2.at[color, c], r2.at[color, c], r2b.at[color, c], 0, HD)
                q_out[blk, core, half, color, : R // 2] = top
                q_out[blk, core, half, color, R // 2 :] = low
            q_share(c).start()

        @pl.when(i == KI + 4)
        def _():
            for color in range(2):
                for d in range(2):
                    k_second(color, 1, d).wait_recv()
                top, low = total_of(kst2.at[color], kr2.at[color], kr2b.at[color], 0, HD)
                kfin[color, :32] = top
                kfin[color, 32:] = low
            for n in range(len(PEERS)):
                key_send(n).start()
            k_out[k_blk, core, k_slot] = kfin[x // 2]
            total = ssq_own[...]
            for n in range(len(PEERS)):
                square_send(n).wait_recv()
                total = total + ssq_in[n]
            ssq_sum[...] = total
            square_share.start()
            put_squares(ssq_sum, core)

        @pl.when(i == KI + 6)
        def _():
            for n in range(len(PEERS)):
                key_send(n).wait_recv()
            k_share.start()

        return carry

    lax.fori_loop(0, LAST, body, 0)
    k_share.wait_recv()
    square_share.wait_recv()
    put_squares(ssq_far, 1 - core)

    def drain(c, carry):
        for color, d in both:
            for stage in range(2):
                q_first(c, color, stage, d).wait_send()
                q_second(c, color, stage, d).wait_send()
        q_share(c).wait()
        return carry

    for color, d in both:
        for stage in range(2):
            k_first(color, stage, d).wait_send()
            k_second(color, stage, d).wait_send()
    for copy in gathers:
        copy.wait_send()
    for n in range(len(PEERS)):
        key_send(n).wait_send()
        square_send(n).wait_send()
    k_share.wait_send()
    square_share.wait_send()
    lax.fori_loop(0, CH, drain, 0)


def project(tokens, gain, query_weight, key_weight):
    dma = pltpu.SemaphoreType.DMA
    vmem = pl.BlockSpec(memory_space=pltpu.VMEM)
    hbm = pl.BlockSpec(memory_space=pl.ANY)
    n = len(PEERS)
    k = tokens.shape[1]
    return pl.pallas_call(
        project_kernel,
        name="project",
        out_shape=(
            jax.ShapeDtypeStruct((4, 2, 2, 2, R, HD), BF16),
            jax.ShapeDtypeStruct((4, 2, 4, 64, HD), BF16),
            jax.ShapeDtypeStruct((16, 128), F32),
        ),
        in_specs=[hbm, vmem, hbm, hbm],
        out_specs=(vmem, vmem, vmem),
        scratch_shapes=[
            pltpu.VMEM((CH, R, k), BF16),
            pltpu.VMEM((CH, R, k), BF16),
            pltpu.VMEM((16, k, 256), BF16),
            pltpu.VMEM((k, 256), BF16),
            pltpu.VMEM((2, CH, 4, R, 512), BF16),
            pltpu.VMEM((2, CH, 2, R, 512), BF16),
            pltpu.VMEM((2, CH, R, 512), BF16),
            pltpu.VMEM((2, CH, 4, R, HD), BF16),
            pltpu.VMEM((2, CH, 2, R, HD), BF16),
            pltpu.VMEM((2, CH, R, HD), BF16),
            pltpu.VMEM((CH * R, 256), BF16),
            pltpu.VMEM((2, 4, 64, 512), BF16),
            pltpu.VMEM((2, 2, 64, 512), BF16),
            pltpu.VMEM((2, 64, 512), BF16),
            pltpu.VMEM((2, 4, 64, HD), BF16),
            pltpu.VMEM((2, 2, 64, HD), BF16),
            pltpu.VMEM((2, 64, HD), BF16),
            pltpu.VMEM((2, 64, HD), BF16),
            pltpu.VMEM((CH, 128), F32),
            pltpu.VMEM((n, CH, 128), F32),
            pltpu.VMEM((CH, 128), F32),
            pltpu.VMEM((CH, 128), F32),
            dma((3,)), dma((16,)), dma((6,)), dma((6,)),
            dma((CH, 2, 2, 2, 2)), dma((CH, 2, 2, 2, 2)),
            dma((2, 2, 2, 2)), dma((2, 2, 2, 2)),
            dma((n,)), dma((n,)), dma((n,)), dma((n,)),
            dma((CH,)), dma((CH,)), dma((2,)), dma((2,)),
        ],
        compiler_params=pltpu.CompilerParams(
            collective_id=0, has_side_effects=True, vmem_limit_bytes=56 * 1024 * 1024
        ),
    )(tokens, gain, query_weight, key_weight)


QB = 128
KB = 256
WIN = 384
QWIN = 144
OWN = NS // 2
SCALE = math.log2(math.e) / math.sqrt(HD)
NT = (((1,), (1,)), ((), ()))


def attention_kernel(
    q_ref, k_ref, ssq_ref, tab_ref, doc_ref, span_ref, span_smem, out_hbm,
    keys, marks, qs, sbuf, km, tot, cnt, obuf, sem,
):
    core = lax.axis_index(CORE)
    docs = doc_ref[...]
    spans = span_ref[...]

    def below(a, v):
        return jnp.sum(jnp.where(a < v, 1.0, 0.0)).astype(jnp.int32)

    c1, c2, c3 = below(docs, 1), below(docs, 2), below(docs, 3)
    mid = below(spans, OWN)
    eye = lax.broadcasted_iota(jnp.int32, (QB, QB), 0) == lax.broadcasted_iota(jnp.int32, (QB, QB), 1)
    low_lanes = lax.broadcasted_iota(jnp.int32, (QB, HD), 1) < HD // 2

    def start_of(i):
        return jnp.where(i >= c3, c3, jnp.where(i >= c2, c2, jnp.where(i >= c1, c1, 0)))

    def tables(b):
        t = tab_ref[pl.ds(pl.multiple_of(b * QB, QB), QB), :]
        turned = pltpu.roll(t, HD // 2, 1)
        row = lax.rsqrt(ssq_ref[pl.ds(b, 1), :] / D + 1e-05)
        col = jnp.sum(jnp.where(eye, row, 0.0), axis=1, keepdims=True)
        return jnp.where(low_lanes, t, turned) * col, jnp.where(low_lanes, -turned, t) * col

    def turn(v, cosine, sine):
        return v * cosine + pltpu.roll(v, HD // 2, 1) * sine

    def make_keys(b, carry):
        cosine, sine = tables(b)
        rows = pl.ds(pl.multiple_of(b * QB, QB), QB)
        keys[rows, :] = turn(k_ref[rows, :].astype(F32), cosine, sine).astype(BF16)
        return carry

    lax.fori_loop(0, TOKENS // QB, make_keys, 0)

    def base_of(kb):
        return span_smem[kb * KB] // 128 * 128

    def make_marks(kb, carry):
        ids = lax.broadcasted_iota(jnp.int32, (WIN, 128), 0) + base_of(kb)
        for half in range(2):
            row = span_ref[pl.ds(kb * 2 + half, 1), :]
            marks[kb, :, half * 128 : (half + 1) * 128] = jnp.where(ids == row, 1.0, 0.0).astype(BF16)
        return carry

    lax.fori_loop(0, TOKENS // KB, make_marks, 0)
    tot[...] = jnp.zeros_like(tot)
    cnt[...] = jnp.zeros_like(cnt)
    ones = jnp.ones((QB, 128), BF16)

    def block(qb, carry):
        cosine, sine = tables(qb)
        for h in range(2):
            v = q_ref[qb, h * QB : (h + 1) * QB, :].astype(F32)
            qs[h * QB : (h + 1) * QB, :] = (turn(v, cosine, sine) * SCALE).astype(BF16)
        first = qb * QB
        kb0 = start_of(first) // KB
        kb1 = qb // 2
        rows = lax.broadcasted_iota(jnp.int32, (QB, 1), 0) + first
        begin = start_of(rows)
        query = qs[...]

        def score(kb, peak):
            block_keys = keys[pl.ds(pl.multiple_of(kb * KB, KB), KB), :]
            s = lax.dot_general(query, block_keys, NT, preferred_element_type=F32)
            cols = lax.broadcasted_iota(jnp.int32, (QB, KB), 1) + kb * KB
            seen = (cols <= rows) & (cols >= begin)
            s0 = jnp.where(seen, s[:QB], -1e30)
            s1 = jnp.where(seen, s[QB:], -1e30)
            sbuf[kb - kb0, :QB, :] = s0
            sbuf[kb - kb0, QB:, :] = s1
            top = jnp.concatenate([jnp.maximum(s0[:, :128], s0[:, 128:]), jnp.maximum(s1[:, :128], s1[:, 128:])], 0)
            return jnp.maximum(peak, top)

        peak = lax.fori_loop(kb0, kb1 + 1, score, jnp.full((2 * QB, 128), -1e30, F32))
        peak = jnp.max(peak, axis=1, keepdims=True)
        km[...] = jnp.zeros_like(km)

        def mass(kb, total):
            e = jnp.exp2(sbuf[kb - kb0] - peak)
            got = lax.dot_general(e.astype(BF16), marks[kb], NT, preferred_element_type=F32)
            lanes = pl.ds(pl.multiple_of(base_of(kb), 128), WIN)
            km[:, lanes] = km[:, lanes] + got
            return total + e[:, :128] + e[:, 128:]

        total = lax.fori_loop(kb0, kb1 + 1, mass, jnp.zeros((2 * QB, 128), F32))
        scale = 1.0 / jnp.sum(total, axis=1, keepdims=True)
        lead = jnp.maximum(span_smem[first] - core * OWN, 0) // 8 * 8
        ids = lax.broadcasted_iota(jnp.int32, (QWIN, QB), 0) + lead
        row = span_ref[pl.ds(qb, 1), :] - core * OWN
        pick = jnp.where(ids == row, 1.0, 0.0).astype(BF16)
        at = pl.ds(pl.multiple_of(lead, 8), QWIN)
        for h in range(2):
            for j in range(4):
                lanes = slice(j * 256, (j + 1) * 256)
                part = (km[h * QB : (h + 1) * QB, lanes] * scale[h * QB : (h + 1) * QB]).astype(BF16)
                tot[h, at, lanes] = tot[h, at, lanes] + jnp.dot(pick, part, preferred_element_type=F32)
        cnt[at, :] = cnt[at, :] + jnp.dot(pick, ones, preferred_element_type=F32)
        return carry

    lo = core * mid // QB
    hi = jnp.where(core == 0, (mid + QB - 1) // QB, TOKENS // QB)
    lax.fori_loop(lo, hi, block, 0)

    step_rows = 64

    def out_copy(n):
        rows = pl.ds(n * step_rows, step_rows)
        return pltpu.make_async_copy(obuf.at[rows], out_hbm.at[rows], sem.at[n])

    for n in range(OWN // step_rows):
        rows = slice(n * step_rows, (n + 1) * step_rows)
        share = 1.0 / cnt[rows, :]
        for h in range(2):
            for j in range(NS // 128):
                lanes = slice(j * 128, (j + 1) * 128)
                obuf[rows, h, lanes] = jnp.log(tot[h, rows, lanes] * share + 1e-06)
        out_copy(n).start()
    for n in range(OWN // step_rows):
        out_copy(n).wait()


def attention(q, k, ssq, table, documents, span_ids):
    vmem = pl.BlockSpec(memory_space=pltpu.VMEM)
    return pl.pallas_call(
        attention_kernel,
        name="attention",
        out_shape=jax.ShapeDtypeStruct((OWN, 2, NS), F32),
        in_specs=[vmem] * 6 + [pl.BlockSpec(memory_space=pltpu.SMEM)],
        out_specs=pl.BlockSpec(memory_space=pl.ANY),
        scratch_shapes=[
            pltpu.VMEM((TOKENS, HD), BF16),
            pltpu.VMEM((TOKENS // KB, WIN, KB), BF16),
            pltpu.VMEM((2 * QB, HD), BF16),
            pltpu.VMEM((6, 2 * QB, KB), F32),
            pltpu.VMEM((2 * QB, NS + 256), F32),
            pltpu.VMEM((2, OWN + QWIN, NS), F32),
            pltpu.VMEM((OWN + QWIN, 128), F32),
            pltpu.VMEM((OWN, 2, NS), F32),
            pltpu.SemaphoreType.DMA((8,)),
        ],
        compiler_params=pltpu.CompilerParams(vmem_limit_bytes=40 * 1024 * 1024),
    )(q, k, ssq, table, documents.reshape(16, 128), span_ids.reshape(16, 128), span_ids)


def angle_table():
    i = np.arange(HD // 2, dtype=np.float64)
    f = 500000.0 ** (-i / (HD // 2))
    w = 2.0 * np.pi / f
    s = (8192.0 / w - 1.0) / 3.0
    f = np.where(w < 2048.0, f, np.where(w > 8192.0, f / 8.0, (1.0 - s) * f / 8.0 + s * f))
    phase = np.arange(TOKENS, dtype=np.float64)[:, None] * f[None, :]
    return np.concatenate([np.cos(phase), np.sin(phase)], axis=1).astype(np.float32)


def local(tokens, norm_gain, query_weight, key_weight, documents, span_ids):
    q, k, ssq = project(tokens, norm_gain.reshape(1, -1), query_weight, key_weight)
    table = jnp.asarray(angle_table())
    return attention(
        q.reshape(16, 2 * QB, HD), k.reshape(TOKENS, HD), ssq, table, documents, span_ids
    )


def solution(mesh):
    finer = Mesh(
        mesh.devices.reshape(mesh.shape["blk"], 4, 4, mesh.shape["kv"]),
        (Y, X, Z, CORE),
    )
    return jax.shard_map(
        local,
        mesh=finer,
        in_specs=(P((Y, CORE), MP), P(MP), P(MP, Y), P(MP, Y), P(), P()),
        out_specs=P(CORE, BLK_MP, None),
        check_vma=False,
    )
```

time: 227 us -> 107 us (0.47)
  Pallas kernels: 0 us -> 101 us
  waiting for transfers between devices: 75.2 us -> 0 us
  matrix products: 48.8 us -> 0 us
  blocking collectives: 27.8 us -> 0 us
  local copies, waits for them, and re-layouts: 24 us -> 4.33 us
  starting transfers between devices: 19.1 us -> 0 us
  other arithmetic: 17.4 us -> 0 us
  between operations: 13.7 us -> 0.05 us
    pallas_call x0 -> x2, Pallas kernels: none -> 101 us  [the longest x1 78 us: project(): pl.pallas_call(project_kernel, name='project', out_shape=(jax.ShapeDtypeS...]
    reduce_scatter x1 -> x0, waiting for transfers between devices: 56 us -> none  [local(): lax.psum_scatter(jnp.transpose(product.reshape(half_rows, lax.axis_size(M...]
    dot_general x3 -> x0, matrix products: 35.1 us -> none  [the longest x1 18.7 us: local(): jnp.einsum('qa,hqs->ahs', query_onehot, key_mass, preferred_element_type=...]
    all_to_all x3 -> x0, waiting for transfers between devices: 19.2 us -> none  [the longest x1 9.65 us: sent_and_summed(): blocks = lax.all_to_all(split_up(array, dim, peers), axis, 0, 0, tiled=True)]
    all_to_all x3 -> x0, starting transfers between devices: 19.1 us -> none  [the longest x2 15.5 us: copy_for_each(): return lax.all_to_all(copies, axis, split_axis=0, concat_axis=0, tiled=True)]
    psum x2 -> x0, blocking collectives: 19 us -> none  [by_axis(): array = lax.psum(array, axis)]
    sub x1 -> x0, matrix products: 13.7 us -> none  [local(): weights = jnp.exp(jnp.where(visible[None], scores - peak_score, -jnp.inf))]
    dot_general x1 -> x0, local copies, waits for them, and re-layouts: 11.9 us -> none  [local(): jnp.dot(gathered, query_weight, preferred_element_type=jnp.float32)]
  transfers between devices with their start and end apart: 4 -> 0, of which waited for: 3 -> 0; matrix products, arithmetic and copies ran while one was open for 13% -> 0% of each run, Pallas kernels for 0% -> 0%
where the time goes in v1:
time: 107 us; the launch traced here: 106 us
  Pallas kernels  101 us (94%)
  local copies, waits for them, and re-layouts  4.33 us (4%)
    pallas_call x1, Pallas kernels, project(): pl.pallas_call(project_kernel, name='project', out_shape=(jax.ShapeDtypeS...  78 us
    pallas_call x1, Pallas kernels, attention(): pl.pallas_call(attention_kernel, name='attention', out_shape=jax.ShapeDty...  23.1 us
    unnamed x12, local copies, waits for them, and re-layouts  2.97 us

profile of v1, /device:TPU:1, one launch (start us, length us, event | category | flops | bytes accessed | tf_op | source)
XLA Modules:
  0.0 105.6 jit_solution(12228553063038115454)
XLA Ops:
  0.0 0.0 copy-start
  0.0 0.0 copy-start.3
  0.0 0.0 copy-start.4
  0.0 1.4 %reshape.15.gain_ref = bf16[1,1024]{1,0:T(2,128)(2,1)} reshape(bf16[1024]{0:T(1024)(128)(2,1)} %param.8) | data formatting | bytes 4096 | tf_op jit(solution)/shard_map/reshape | solution.py:635
  1.4 78.0 %project.1 = (bf16[4,2,2,2,128,128]{5,4,3,2,1,0:T(8,128)(2,1)}, bf16[4,2,4,64,128]{4,3,2,1,0:T(8,128)(2,1)}, f32[16,128]{1,0:T(8,128)}) custom-call(bf16[256,1024]{1,0:T(8,128)(2,1)} %tok_hbm.1, bf16[1,1024]{1,0:T(2,128)(2,1)} %reshape.15.gain_ref, bf16[1024,4096]{1,0:T(8,128)(2,1)} %w_hbm.1, bf16[1024,256]{1,0:T(8,128)(2,1)} %kw_hbm.1), custom_call_target="tpu_custom_call" | custom-call | tf_op jit(solution)/shard_map/project/pallas_call | solution.py:423
  79.4 0.0 copy-done
  79.4 0.0 copy-done.3
  79.4 0.0 copy-done.4
  79.4 0.0 copy-start.1
  79.4 1.2 %copy-done.1 = bf16[4,2,2,2,128,128]{5,4,3,2,1,0:T(8,128)(2,1)S(1)} copy-done((bf16[4,2,2,2,128,128]{5,4,3,2,1,0:T(8,128)(2,1)S(1)}, bf16[4,2,2,2,128,128]{5,4,3,2,1,0:T(8,128)(2,1)}, u32[]{:S(2)}) %copy-start.1) | copy-done | bytes 1048600
  80.7 0.0 copy-start.2
  80.7 1.0 copy-done.2
  81.7 0.0 copy-start.5
  81.7 0.7 copy-done.5
  82.4 23.1 %attention.1 = f32[512,2,1024]{2,1,0:T(2,128)} custom-call(bf16[16,256,128]{2,1,0:T(8,128)(2,1)S(1)} %bitcast.4, bf16[2048,128]{1,0:T(8,128)(2,1)S(1)} %bitcast.5, f32[16,128]{1,0:T(8,128)S(1)} %copy-done.5, f32[2048,128]{1,0:T(8,128)S(1)} %copy-done, s32[16,128]{1,0:T(8,128)S(1)} %bitcast.7, s32[16,128]{1,0:T(8,128)S(1)} %bitcast.6, s32[2048]{0:T(1024)S(1)} %copy-done.3), custom_call_target="tpu_custom_call" | custom-call | tf_op jit(solution)/shard_map/attention/pallas_call | solution.py:603
Async XLA Ops:
  0.0 79.4 %copy-start = (f32[2048,128]{1,0:T(8,128)S(1)}, f32[2048,128]{1,0:T(8,128)}, u32[]{:S(2)}) copy-start(f32[2048,128]{1,0:T(8,128)} %constant.2.clone.tab_ref) | copy-start | bytes 3145732
  0.0 79.4 %copy-start.3 = (s32[2048]{0:T(1024)S(1)}, s32[2048]{0:T(1024)}, u32[]{:S(2)}) copy-start(s32[2048]{0:T(1024)} %span_smem.1) | copy-start | bytes 24580
  0.0 79.4 %copy-start.4 = (s32[2048]{0:T(1024)S(1)}, s32[2048]{0:T(1024)}, u32[]{:S(2)}) copy-start(s32[2048]{0:T(1024)} %param.11) | copy-start | bytes 24580
  79.4 1.2 %copy-start.1 = (bf16[4,2,2,2,128,128]{5,4,3,2,1,0:T(8,128)(2,1)S(1)}, bf16[4,2,2,2,128,128]{5,4,3,2,1,0:T(8,128)(2,1)}, u32[]{:S(2)}) copy-start(bf16[4,2,2,2,128,128]{5,4,3,2,1,0:T(8,128)(2,1)} %get-tuple-element.8) | copy-start | bytes 3145732
  80.7 1.0 copy-start.2
  81.7 0.7 copy-start.5

commit v2 on v1

--- a/solution.py
+++ b/solution.py
@@ -25,6 +25,7 @@
 R = 128
 KI = 4
 LAST = CH + 4
+WS = 8
 SLOT_A = {2: 0, 1: 2, 3: 1, 0: 3}
 SLOT_B = {2: 1, 1: 0, 3: 2, 0: 3}
 ORDER = (2, 1, 3, 0)
@@ -109,22 +110,21 @@
     def tok_load(p):
         return pltpu.make_async_copy(tok_hbm.at[pl.ds(p * R, R)], tok.at[p], load_sem.at[p])
 
-    def w_load(ox, oz):
-        col = (step(x, ox) * 4 + step(z, oz)) * 256
-        return pltpu.make_async_copy(
-            w_hbm.at[:, pl.ds(pl.multiple_of(col, 256), 256)], wbuf.at[ox * 4 + oz], w_sem.at[ox * 4 + oz]
-        )
+    slab = w_hbm.shape[0] // WS
+
+    def w_load(n):
+        rows = pl.ds(n * slab, slab)
+        return pltpu.make_async_copy(w_hbm.at[rows], wbuf.at[rows], w_sem.at[n])
 
     kw_load = pltpu.make_async_copy(kw_hbm, kwbuf, load_sem.at[2])
     for p in range(2):
         tok_load(p).start()
-    for ox in ORDER:
-        for oz in ORDER:
-            w_load(ox, oz).start()
+    for n in range(WS):
+        w_load(n).start()
     kw_load.start()
 
     def scale(p):
-        xs[p] = (tok[p].astype(F32) * gain_ref[...].astype(F32)).astype(BF16)
+        xs[p * R : (p + 1) * R] = (tok[p].astype(F32) * gain_ref[...].astype(F32)).astype(BF16)
 
     def gather(n, src, dst, by):
         return pltpu.make_async_remote_copy(
@@ -252,34 +252,37 @@
             for p in range(4, 8):
                 scale(p)
 
-        @pl.when(i < CH)
-        def _():
-            lhs = xs[i]
+        @pl.when(i == 0)
+        def _():
+            for n in range(WS):
+                w_load(n).wait()
+
+        @pl.when((i < CH) & (lax.rem(i, 2) == 0))
+        def _():
+            lhs = xs[pl.ds(pl.multiple_of(i * R, 2 * R), 2 * R), :]
             for n, ox in enumerate(ORDER):
                 for oz in ORDER:
-                    @pl.when(i == 0)
-                    def _():
-                        w_load(ox, oz).wait()
-
-                    out = jnp.dot(lhs, wbuf[ox * 4 + oz], preferred_element_type=F32).astype(BF16)
-                    h = R // 2
-                    put(st1.at[0, i], ox, oz * HD, HD, out[:h, :HD], out[h:, :HD])
-                    put(st1.at[1, i], oz, ox * HD, HD, out[:h, HD:], out[h:, HD:])
+                    col = pl.multiple_of((step(x, ox) * 4 + step(z, oz)) * 256, 256)
+                    out = jnp.dot(lhs, wbuf[:, pl.ds(col, 256)], preferred_element_type=F32).astype(BF16)
+                    for u in range(2):
+                        a, b, e = u * R, u * R + R // 2, u * R + R
+                        put(st1.at[0, i + u], ox, oz * HD, HD, out[a:b, :HD], out[b:e, :HD])
+                        put(st1.at[1, i + u], oz, ox * HD, HD, out[a:b, HD:], out[b:e, HD:])
                 if n == 1:
                     q_first(i, 0, 0, 0).start()
                 if n == 2:
                     q_first(i, 0, 0, 1).start()
             for d in range(2):
                 q_first(i, 1, 0, d).start()
-
-        @pl.when(i == KI)
-        def _():
-            kw_load.wait()
+            for color, d in both:
+                q_first(i + 1, color, 0, d).start()
+
+        def key_part(lo, hi):
             eye = lax.broadcasted_iota(jnp.int32, (R, R), 0) == lax.broadcasted_iota(jnp.int32, (R, R), 1)
 
             def one(p, carry):
                 kpart[pl.ds(pl.multiple_of(p * R, R), R), :] = jnp.dot(
-                    xs[p], kwbuf[...], preferred_element_type=F32
+                    xs[pl.ds(pl.multiple_of(p * R, R), R), :], kwbuf[...], preferred_element_type=F32
                 ).astype(BF16)
                 acc = jnp.zeros((R, 128), F32)
                 for j in range(8):
@@ -289,7 +292,20 @@
                 ssq_own[pl.ds(p, 1), :] = jnp.sum(jnp.where(eye, col, 0.0), axis=0, keepdims=True)
                 return carry
 
-            lax.fori_loop(0, CH, one, 0)
+            lax.fori_loop(lo, hi, one, 0)
+
+        @pl.when(i == 1)
+        def _():
+            kw_load.wait()
+            key_part(0, 2)
+
+        @pl.when(i == 3)
+        def _():
+            key_part(2, 4)
+
+        @pl.when(i == KI)
+        def _():
+            key_part(4, CH)
             for ox in range(4):
                 for oz in range(4):
                     row = (step(x, ox) * 4 + step(z, oz)) * 64
@@ -417,7 +433,7 @@
 def project(tokens, gain, query_weight, key_weight):
     dma = pltpu.SemaphoreType.DMA
     vmem = pl.BlockSpec(memory_space=pltpu.VMEM)
-    hbm = pl.BlockSpec(memory_space=pl.ANY)
+    hbm = pl.BlockSpec(memory_space=pltpu.HBM)
     n = len(PEERS)
     k = tokens.shape[1]
     return pl.pallas_call(
@@ -432,8 +448,8 @@
         out_specs=(vmem, vmem, vmem),
         scratch_shapes=[
             pltpu.VMEM((CH, R, k), BF16),
-            pltpu.VMEM((CH, R, k), BF16),
-            pltpu.VMEM((16, k, 256), BF16),
+            pltpu.VMEM((CH * R, k), BF16),
+            pltpu.VMEM((k, query_weight.shape[1]), BF16),
             pltpu.VMEM((k, 256), BF16),
             pltpu.VMEM((2, CH, 4, R, 512), BF16),
             pltpu.VMEM((2, CH, 2, R, 512), BF16),
@@ -453,30 +469,32 @@
             pltpu.VMEM((n, CH, 128), F32),
             pltpu.VMEM((CH, 128), F32),
             pltpu.VMEM((CH, 128), F32),
-            dma((3,)), dma((16,)), dma((6,)), dma((6,)),
+            dma((3,)), dma((WS,)), dma((6,)), dma((6,)),
             dma((CH, 2, 2, 2, 2)), dma((CH, 2, 2, 2, 2)),
             dma((2, 2, 2, 2)), dma((2, 2, 2, 2)),
             dma((n,)), dma((n,)), dma((n,)), dma((n,)),
             dma((CH,)), dma((CH,)), dma((2,)), dma((2,)),
         ],
         compiler_params=pltpu.CompilerParams(
-            collective_id=0, has_side_effects=True, vmem_limit_bytes=56 * 1024 * 1024
+            collective_id=0, has_side_effects=True, vmem_limit_bytes=54 * 1024 * 1024
         ),
     )(tokens, gain, query_weight, key_weight)
 
 
-QB = 128
+SUB = 128
+QB = 256
 KB = 256
 WIN = 384
-QWIN = 144
+PARTS = ((0, 144), (144, 128))
 OWN = NS // 2
+GROUP = 64
 SCALE = math.log2(math.e) / math.sqrt(HD)
 NT = (((1,), (1,)), ((), ()))
 
 
 def attention_kernel(
     q_ref, k_ref, ssq_ref, tab_ref, doc_ref, span_ref, span_smem, out_hbm,
-    keys, marks, qs, sbuf, km, tot, cnt, obuf, sem,
+    keys, marks, qs, sbuf, peaks, sums, km, tot, cnt, obuf, sem,
 ):
     core = lax.axis_index(CORE)
     docs = doc_ref[...]
@@ -487,14 +505,16 @@
 
     c1, c2, c3 = below(docs, 1), below(docs, 2), below(docs, 3)
     mid = below(spans, OWN)
-    eye = lax.broadcasted_iota(jnp.int32, (QB, QB), 0) == lax.broadcasted_iota(jnp.int32, (QB, QB), 1)
-    low_lanes = lax.broadcasted_iota(jnp.int32, (QB, HD), 1) < HD // 2
+    lo = core * mid // QB
+    hi = jnp.where(core == 0, (mid + QB - 1) // QB, TOKENS // QB)
+    eye = lax.broadcasted_iota(jnp.int32, (SUB, SUB), 0) == lax.broadcasted_iota(jnp.int32, (SUB, SUB), 1)
+    low_lanes = lax.broadcasted_iota(jnp.int32, (SUB, HD), 1) < HD // 2
 
     def start_of(i):
         return jnp.where(i >= c3, c3, jnp.where(i >= c2, c2, jnp.where(i >= c1, c1, 0)))
 
     def tables(b):
-        t = tab_ref[pl.ds(pl.multiple_of(b * QB, QB), QB), :]
+        t = tab_ref[pl.ds(pl.multiple_of(b * SUB, SUB), SUB), :]
         turned = pltpu.roll(t, HD // 2, 1)
         row = lax.rsqrt(ssq_ref[pl.ds(b, 1), :] / D + 1e-05)
         col = jnp.sum(jnp.where(eye, row, 0.0), axis=1, keepdims=True)
@@ -503,98 +523,119 @@
     def turn(v, cosine, sine):
         return v * cosine + pltpu.roll(v, HD // 2, 1) * sine
 
-    def make_keys(b, carry):
-        cosine, sine = tables(b)
-        rows = pl.ds(pl.multiple_of(b * QB, QB), QB)
-        keys[rows, :] = turn(k_ref[rows, :].astype(F32), cosine, sine).astype(BF16)
-        return carry
-
-    lax.fori_loop(0, TOKENS // QB, make_keys, 0)
-
     def base_of(kb):
         return span_smem[kb * KB] // 128 * 128
 
-    def make_marks(kb, carry):
+    def prepare(kb, carry):
         ids = lax.broadcasted_iota(jnp.int32, (WIN, 128), 0) + base_of(kb)
         for half in range(2):
-            row = span_ref[pl.ds(kb * 2 + half, 1), :]
+            b = kb * 2 + half
+            cosine, sine = tables(b)
+            rows = pl.ds(pl.multiple_of(b * SUB, SUB), SUB)
+            keys[rows, :] = turn(k_ref[rows, :].astype(F32), cosine, sine).astype(BF16)
+            row = span_ref[pl.ds(b, 1), :]
             marks[kb, :, half * 128 : (half + 1) * 128] = jnp.where(ids == row, 1.0, 0.0).astype(BF16)
         return carry
 
-    lax.fori_loop(0, TOKENS // KB, make_marks, 0)
+    lax.fori_loop(start_of(lo * QB) // KB, hi, prepare, 0)
     tot[...] = jnp.zeros_like(tot)
     cnt[...] = jnp.zeros_like(cnt)
     ones = jnp.ones((QB, 128), BF16)
 
-    def block(qb, carry):
-        cosine, sine = tables(qb)
-        for h in range(2):
-            v = q_ref[qb, h * QB : (h + 1) * QB, :].astype(F32)
-            qs[h * QB : (h + 1) * QB, :] = (turn(v, cosine, sine) * SCALE).astype(BF16)
-        first = qb * QB
-        kb0 = start_of(first) // KB
-        kb1 = qb // 2
-        rows = lax.broadcasted_iota(jnp.int32, (QB, 1), 0) + first
-        begin = start_of(rows)
-        query = qs[...]
-
-        def score(kb, peak):
-            block_keys = keys[pl.ds(pl.multiple_of(kb * KB, KB), KB), :]
-            s = lax.dot_general(query, block_keys, NT, preferred_element_type=F32)
-            cols = lax.broadcasted_iota(jnp.int32, (QB, KB), 1) + kb * KB
-            seen = (cols <= rows) & (cols >= begin)
-            s0 = jnp.where(seen, s[:QB], -1e30)
-            s1 = jnp.where(seen, s[QB:], -1e30)
-            sbuf[kb - kb0, :QB, :] = s0
-            sbuf[kb - kb0, QB:, :] = s1
-            top = jnp.concatenate([jnp.maximum(s0[:, :128], s0[:, 128:]), jnp.maximum(s1[:, :128], s1[:, 128:])], 0)
-            return jnp.maximum(peak, top)
-
-        peak = lax.fori_loop(kb0, kb1 + 1, score, jnp.full((2 * QB, 128), -1e30, F32))
-        peak = jnp.max(peak, axis=1, keepdims=True)
-        km[...] = jnp.zeros_like(km)
-
-        def mass(kb, total):
-            e = jnp.exp2(sbuf[kb - kb0] - peak)
-            got = lax.dot_general(e.astype(BF16), marks[kb], NT, preferred_element_type=F32)
-            lanes = pl.ds(pl.multiple_of(base_of(kb), 128), WIN)
-            km[:, lanes] = km[:, lanes] + got
-            return total + e[:, :128] + e[:, 128:]
-
-        total = lax.fori_loop(kb0, kb1 + 1, mass, jnp.zeros((2 * QB, 128), F32))
-        scale = 1.0 / jnp.sum(total, axis=1, keepdims=True)
-        lead = jnp.maximum(span_smem[first] - core * OWN, 0) // 8 * 8
-        ids = lax.broadcasted_iota(jnp.int32, (QWIN, QB), 0) + lead
-        row = span_ref[pl.ds(qb, 1), :] - core * OWN
-        pick = jnp.where(ids == row, 1.0, 0.0).astype(BF16)
-        at = pl.ds(pl.multiple_of(lead, 8), QWIN)
-        for h in range(2):
-            for j in range(4):
-                lanes = slice(j * 256, (j + 1) * 256)
-                part = (km[h * QB : (h + 1) * QB, lanes] * scale[h * QB : (h + 1) * QB]).astype(BF16)
-                tot[h, at, lanes] = tot[h, at, lanes] + jnp.dot(pick, part, preferred_element_type=F32)
-        cnt[at, :] = cnt[at, :] + jnp.dot(pick, ones, preferred_element_type=F32)
-        return carry
-
-    lo = core * mid // QB
-    hi = jnp.where(core == 0, (mid + QB - 1) // QB, TOKENS // QB)
-    lax.fori_loop(lo, hi, block, 0)
-
-    step_rows = 64
-
     def out_copy(n):
-        rows = pl.ds(n * step_rows, step_rows)
+        rows = pl.ds(pl.multiple_of(n * GROUP, GROUP), GROUP)
         return pltpu.make_async_copy(obuf.at[rows], out_hbm.at[rows], sem.at[n])
 
-    for n in range(OWN // step_rows):
-        rows = slice(n * step_rows, (n + 1) * step_rows)
+    def finish(n, carry):
+        rows = pl.ds(pl.multiple_of(n * GROUP, GROUP), GROUP)
         share = 1.0 / cnt[rows, :]
         for h in range(2):
             for j in range(NS // 128):
                 lanes = slice(j * 128, (j + 1) * 128)
                 obuf[rows, h, lanes] = jnp.log(tot[h, rows, lanes] * share + 1e-06)
         out_copy(n).start()
-    for n in range(OWN // step_rows):
+        return carry
+
+    def block(qb, done):
+        first = qb * QB
+        for u in range(2):
+            cosine, sine = tables(qb * 2 + u)
+            for h in range(2):
+                v = q_ref[qb * 2 + u, h * SUB : (h + 1) * SUB, :].astype(F32)
+                at = h * QB + u * SUB
+                qs[at : at + SUB, :] = (turn(v, cosine, sine) * SCALE).astype(BF16)
+        kb0 = start_of(first) // KB
+        last = span_smem[first + QB - 1]
+        tile0 = base_of(kb0) // 256
+
+        peaks[...] = jnp.full_like(peaks, -1e30)
+
+        def score(kb, carry):
+            block_keys = keys[pl.ds(pl.multiple_of(kb * KB, KB), KB), :]
+            s = lax.dot_general(qs[...], block_keys, NT, preferred_element_type=F32)
+            cols = lax.broadcasted_iota(jnp.int32, (SUB, KB), 1) + kb * KB
+            for u in range(2):
+                rows = lax.broadcasted_iota(jnp.int32, (SUB, 1), 0) + (first + u * SUB)
+                seen = (cols <= rows) & (cols >= start_of(rows))
+                for h in range(2):
+                    at = slice(h * QB + u * SUB, h * QB + (u + 1) * SUB)
+                    part = jnp.where(seen, s[at], -1e30)
+                    sbuf[kb - kb0, at, :] = part
+                    peaks[at, :] = jnp.maximum(peaks[at, :], jnp.maximum(part[:, :128], part[:, 128:]))
+            return carry
+
+        lax.fori_loop(kb0, qb + 1, score, 0)
+        peak = jnp.max(peaks[...], axis=1, keepdims=True)
+        sums[...] = jnp.zeros_like(sums)
+
+        def clear(t, carry):
+            km[:, pl.ds(pl.multiple_of(t * 256, 256), 256)] = jnp.zeros((2 * QB, 256), F32)
+            return carry
+
+        lax.fori_loop(tile0, jnp.maximum(base_of(qb) + WIN - 1, last) // 256 + 1, clear, 0)
+
+        def mass(kb, carry):
+            e = jnp.exp2(sbuf[kb - kb0] - peak)
+            sums[...] = sums[...] + e[:, :128] + e[:, 128:]
+            got = lax.dot_general(e.astype(BF16), marks[kb], NT, preferred_element_type=F32)
+            lanes = pl.ds(pl.multiple_of(base_of(kb), 128), WIN)
+            km[:, lanes] = km[:, lanes] + got
+            return carry
+
+        lax.fori_loop(kb0, qb + 1, mass, 0)
+        scale = 1.0 / jnp.sum(sums[...], axis=1, keepdims=True)
+        lead = jnp.maximum(span_smem[first] - core * OWN, 0) // 8 * 8
+        row = jnp.concatenate([span_ref[pl.ds(qb * 2, 1), :], span_ref[pl.ds(qb * 2 + 1, 1), :]], axis=1)
+
+        def gather_part(lo_row, n):
+            ids = lax.broadcasted_iota(jnp.int32, (n, QB), 0) + (lead + lo_row + core * OWN)
+            pick = jnp.where(ids == row, 1.0, 0.0).astype(BF16)
+            at = pl.ds(pl.multiple_of(lead + lo_row, 8), n)
+
+            def tile(t, carry):
+                lanes = pl.ds(pl.multiple_of(t * 256, 256), 256)
+                for h in range(2):
+                    hs = slice(h * QB, (h + 1) * QB)
+                    part = (km[hs, lanes] * scale[hs]).astype(BF16)
+                    tot[h, at, lanes] = tot[h, at, lanes] + jnp.dot(pick, part, preferred_element_type=F32)
+                return carry
+
+            lax.fori_loop(tile0, last // 256 + 1, tile, 0)
+            cnt[at, :] = cnt[at, :] + jnp.dot(pick, ones, preferred_element_type=F32)
+
+        gather_part(*PARTS[0])
+
+        @pl.when(last - core * OWN >= lead + PARTS[1][0])
+        def _():
+            gather_part(*PARTS[1])
+
+        ready = (span_smem[jnp.minimum(first + QB, TOKENS - 1)] - core * OWN) // GROUP
+        ready = jnp.where(qb + 1 == hi, OWN // GROUP, ready)
+        lax.fori_loop(done, ready, finish, 0)
+        return ready
+
+    lax.fori_loop(lo, hi, block, 0)
+    for n in range(OWN // GROUP):
         out_copy(n).wait()
 
 
@@ -611,13 +652,15 @@
             pltpu.VMEM((TOKENS // KB, WIN, KB), BF16),
             pltpu.VMEM((2 * QB, HD), BF16),
             pltpu.VMEM((6, 2 * QB, KB), F32),
+            pltpu.VMEM((2 * QB, 128), F32),
+            pltpu.VMEM((2 * QB, 128), F32),
             pltpu.VMEM((2 * QB, NS + 256), F32),
-            pltpu.VMEM((2, OWN + QWIN, NS), F32),
-            pltpu.VMEM((OWN + QWIN, 128), F32),
+            pltpu.VMEM((2, OWN + 272, NS), F32),
+            pltpu.VMEM((OWN + 272, 128), F32),
             pltpu.VMEM((OWN, 2, NS), F32),
             pltpu.SemaphoreType.DMA((8,)),
         ],
-        compiler_params=pltpu.CompilerParams(vmem_limit_bytes=40 * 1024 * 1024),
+        compiler_params=pltpu.CompilerParams(vmem_limit_bytes=32 * 1024 * 1024),
     )(q, k, ssq, table, documents.reshape(16, 128), span_ids.reshape(16, 128), span_ids)
 
 
@@ -635,7 +678,7 @@
     q, k, ssq = project(tokens, norm_gain.reshape(1, -1), query_weight, key_weight)
     table = jnp.asarray(angle_table())
     return attention(
-        q.reshape(16, 2 * QB, HD), k.reshape(TOKENS, HD), ssq, table, documents, span_ids
+        q.reshape(16, 2 * SUB, HD), k.reshape(TOKENS, HD), ssq, table, documents, span_ids
     )
 
 

time: 107 us -> 100 us (0.935)
  Pallas kernels: 101 us -> 94.1 us
    pallas_call x1, Pallas kernels: 23.1 us -> 17 us  [attention(): pl.pallas_call(attention_kernel, name='attention', out_shape=jax.ShapeDty...]
where the time goes in v2:
time: 100 us; the launch traced here: 98.5 us
  Pallas kernels  94.1 us (94%)
  local copies, waits for them, and re-layouts  4.33 us (4%)
    pallas_call x1, Pallas kernels, project(): pl.pallas_call(project_kernel, name='project', out_shape=(jax.ShapeDtypeS...  77.1 us
    pallas_call x1, Pallas kernels, attention(): pl.pallas_call(attention_kernel, name='attention', out_shape=jax.ShapeDty...  17 us
    unnamed x12, local copies, waits for them, and re-layouts  2.97 us

profile of v2, /device:TPU:1, one launch (start us, length us, event | category | flops | bytes accessed | tf_op | source)
XLA Modules:
  0.0 98.5 jit_solution(1974929418554541712)
XLA Ops:
  0.0 0.0 copy-start
  0.0 0.0 copy-start.3
  0.0 0.0 copy-start.4
  0.0 1.4 %reshape.15.gain_ref = bf16[1,1024]{1,0:T(2,128)(2,1)} reshape(bf16[1024]{0:T(1024)(128)(2,1)} %param.8) | data formatting | bytes 4096 | tf_op jit(solution)/shard_map/reshape | solution.py:678
  1.4 77.1 %project.1 = (bf16[4,2,2,2,128,128]{5,4,3,2,1,0:T(8,128)(2,1)}, bf16[4,2,4,64,128]{4,3,2,1,0:T(8,128)(2,1)}, f32[16,128]{1,0:T(8,128)}) custom-call(bf16[256,1024]{1,0:T(8,128)(2,1)} %tok_hbm.1, bf16[1,1024]{1,0:T(2,128)(2,1)} %reshape.15.gain_ref, bf16[1024,4096]{1,0:T(8,128)(2,1)} %w_hbm.1, bf16[1024,256]{1,0:T(8,128)(2,1)} %kw_hbm.1), custom_call_target="tpu_custom_call" | custom-call | tf_op jit(solution)/shard_map/project/pallas_call | solution.py:439
  78.4 0.0 copy-done
  78.5 0.0 copy-done.3
  78.5 0.0 copy-done.4
  78.5 0.0 copy-start.1
  78.5 1.2 %copy-done.1 = bf16[4,2,2,2,128,128]{5,4,3,2,1,0:T(8,128)(2,1)S(1)} copy-done((bf16[4,2,2,2,128,128]{5,4,3,2,1,0:T(8,128)(2,1)S(1)}, bf16[4,2,2,2,128,128]{5,4,3,2,1,0:T(8,128)(2,1)}, u32[]{:S(2)}) %copy-start.1) | copy-done | bytes 1048600
  79.7 0.0 copy-start.2
  79.7 1.0 %copy-done.2 = bf16[4,2,4,64,128]{4,3,2,1,0:T(8,128)(2,1)S(1)} copy-done((bf16[4,2,4,64,128]{4,3,2,1,0:T(8,128)(2,1)S(1)}, bf16[4,2,4,64,128]{4,3,2,1,0:T(8,128)(2,1)}, u32[]{:S(2)}) %copy-start.2) | copy-done | bytes 524312
  80.7 0.0 copy-start.5
  80.7 0.7 copy-done.5
  81.4 17.0 %attention.1 = f32[512,2,1024]{2,1,0:T(2,128)} custom-call(bf16[16,256,128]{2,1,0:T(8,128)(2,1)S(1)} %bitcast.4, bf16[2048,128]{1,0:T(8,128)(2,1)S(1)} %bitcast.5, f32[16,128]{1,0:T(8,128)S(1)} %copy-done.5, f32[2048,128]{1,0:T(8,128)S(1)} %copy-done, s32[16,128]{1,0:T(8,128)S(1)} %bitcast.7, s32[16,128]{1,0:T(8,128)S(1)} %bitcast.6, s32[2048]{0:T(1024)S(1)} %copy-done.3), custom_call_target="tpu_custom_call" | custom-call | tf_op jit(solution)/shard_map/attention/pallas_call | solution.py:644
Async XLA Ops:
  0.0 78.4 %copy-start = (f32[2048,128]{1,0:T(8,128)S(1)}, f32[2048,128]{1,0:T(8,128)}, u32[]{:S(2)}) copy-start(f32[2048,128]{1,0:T(8,128)} %constant.2.clone.tab_ref) | copy-start | bytes 3145732
  0.0 78.5 %copy-start.3 = (s32[2048]{0:T(1024)S(1)}, s32[2048]{0:T(1024)}, u32[]{:S(2)}) copy-start(s32[2048]{0:T(1024)} %span_smem.1) | copy-start | bytes 24580
  0.0 78.5 %copy-start.4 = (s32[2048]{0:T(1024)S(1)}, s32[2048]{0:T(1024)}, u32[]{:S(2)}) copy-start(s32[2048]{0:T(1024)} %param.11) | copy-start | bytes 24580
  78.5 1.2 %copy-start.1 = (bf16[4,2,2,2,128,128]{5,4,3,2,1,0:T(8,128)(2,1)S(1)}, bf16[4,2,2,2,128,128]{5,4,3,2,1,0:T(8,128)(2,1)}, u32[]{:S(2)}) copy-start(bf16[4,2,2,2,128,128]{5,4,3,2,1,0:T(8,128)(2,1)} %get-tuple-element.8) | copy-start | bytes 3145732
  79.7 1.0 %copy-start.2 = (bf16[4,2,4,64,128]{4,3,2,1,0:T(8,128)(2,1)S(1)}, bf16[4,2,4,64,128]{4,3,2,1,0:T(8,128)(2,1)}, u32[]{:S(2)}) copy-start(bf16[4,2,4,64,128]{4,3,2,1,0:T(8,128)(2,1)} %get-tuple-element.9) | copy-start | bytes 1572868
  80.7 0.7 copy-start.5
